TPU v7x, 32 devices: a whole 2x2x4 slice. The times are simulated.
32 devices in a mesh: beam: 8 (over z, x), tm: 4 (over y, core).
Axes of the slice: x: 2, y: 2, z: 4, core: 2. Of those that a mesh axis runs over, the one named last changes fastest.
Arguments:
- voltages: float32 [8, 2, 2, 64, 8192], P('beam', None, None, 'tm'), may hold values from -20 to 20
- filter_taps: float32 [8, 8192], replicated, may hold values from -2 to 2
Outputs:
- cleaned: float32 [8, 2, 64, 8192], P('beam', None, 'tm')
All inputs are finite; a program needn't handle non-finite values.
Results may differ from a plain program's by a relative error of at most 0.000058.
Values sent between devices are 32-bit elements; how exact they have to be, the bound alone decides.
A program may use at most 64 MiB of HBM per device.

v0:
```python
import math

import jax
import jax.numpy as jnp
from jax import lax
from jax.sharding import PartitionSpec as P

RADIX = 128


def passed_along(x, axis, by):
    devices = lax.axis_size(axis)
    pairs = [(i, i + by) for i in range(devices) if 0 <= i + by < devices]
    return lax.ppermute(x, axis, pairs)


def twiddles(rows_count, cols_count, modulus):
    product = (
        jnp.arange(rows_count, dtype=jnp.int32)[:, None]
        * jnp.arange(cols_count, dtype=jnp.int32)[None, :]
        % modulus
    )
    angles = product.astype(jnp.float32) * (-2.0 * math.pi / modulus)
    return (jnp.cos(angles), jnp.sin(angles))


def complex_apply(form, table_cos, table_sin, real_part, imag_part):

    def apply(table, values):
        return jnp.einsum(form, table, values, precision=lax.Precision.HIGHEST)

    return (
        apply(table_cos, real_part) - apply(table_sin, imag_part),
        apply(table_cos, imag_part) + apply(table_sin, real_part),
    )


def tap_sum(filter_taps, source, count):
    result = filter_taps[0] * source[:, :, 0:count]
    for tap_index in range(1, filter_taps.shape[0]):
        result = result + filter_taps[tap_index] * source[:, :, tap_index : tap_index + count]
    return result


def body(voltages, filter_taps):
    segment = voltages[0]
    frames = segment.shape[2]
    channels = segment.shape[3]
    rim_frames = filter_taps.shape[0] - 1
    zero_rim = jnp.zeros((2, 2, rim_frames, channels), jnp.float32)
    padded = jnp.concatenate([segment, zero_rim], axis=2)
    filtered = tap_sum(filter_taps, padded, frames)
    leading_rows = jnp.concatenate([zero_rim, segment[:, :, :rim_frames]], axis=2)
    partial_value = tap_sum(filter_taps, leading_rows, rim_frames)
    incoming = passed_along(partial_value, "tm", -1)
    filtered = filtered.at[:, :, frames - rim_frames :].add(incoming)
    stride = channels // RADIX
    grid_real = filtered[:, 0].reshape(2, frames, RADIX, stride)
    grid_imag = filtered[:, 1].reshape(2, frames, RADIX, stride)
    cos_first, sin_first = twiddles(RADIX, RADIX, RADIX)
    section_real, section_imag = complex_apply(
        "kn,pfnm->pfmk", cos_first, sin_first, grid_real, grid_imag
    )
    twist_cos, twist_sin = twiddles(stride, RADIX, channels)
    twisted_real = section_real * twist_cos - section_imag * twist_sin
    twisted_imag = section_real * twist_sin + section_imag * twist_cos
    cos_second, sin_second = twiddles(stride, stride, stride)
    spec_real, spec_imag = complex_apply(
        "jm,pfmk->pfjk", cos_second, sin_second, twisted_real, twisted_imag
    )
    powers = ((spec_real * spec_real + spec_imag * spec_imag) / channels).reshape(
        2, frames, channels
    )
    totals = jnp.sum(powers, axis=1)
    channel_sum = lax.psum(totals, ("beam", "tm"))
    all_frames = frames * lax.axis_size("tm")
    all_beams = voltages.shape[0] * lax.axis_size("beam")
    baseline = channel_sum / all_frames / all_beams
    return (powers - baseline[:, None, :])[None]


def solution(mesh):
    placed = (P("beam", None, None, "tm", None), P())
    return jax.shard_map(
        body, mesh=mesh, in_specs=placed, out_specs=P("beam", None, "tm", None), check_vma=False
    )
```

profile of v0, /device:TPU:0, one launch (start us, length us, event | category | flops | bytes accessed | tf_op | source)
XLA Modules:
  0.0 192.7 jit_solution(11164016761553831303)
XLA Ops:
  6.5 0.0 all-reduce.4.cloned.1.call-start
  6.5 2.3 %fusion.100 = (f32[1,8192]{1,0:T(1,128)S(1)}, f32[1,8192]{1,0:T(1,128)S(1)}, f32[1,8192]{1,0:T(1,128)S(1)}, f32[1,8192]{1,0:T(1,128)S(1)}, f32[1,8192]{1,0:T(1,1...) fusion(f32[8,8192]{1,0:T(8,128)} %param.5), kind=kLoop, calls=%fused_computation.126 | loop fusion | bytes 524288 | tf_op jit(solution)/shard_map/slice | solution.py:39
  8.9 3.2 %copy.23 = f32[1,2,2,16,8192]{4,2,3,1,0:T(2,128)S(1)} copy(f32[1,2,2,16,8192]{4,3,2,1,0:T(8,128)} %param.4) | data formatting | bytes 4194304 | tf_op args[0]
  12.1 0.1 slice.135
  12.2 1.6 multiply_add_fusion.2
  13.8 1.3 collective-permute-start
  15.1 7.2 %multiply_add_fusion = f32[2,2,16,8192]{3,1,2,0:T(2,128)S(1)} fusion(f32[2,2,16,8192]{3,1,2,0:T(2,128)S(1)} %bitcast.54, f32[8192]{0:T(1024)S(1)} %bitcast.66, f32[8192]{0:T(1024)S(1)} %bitcast.68, f32[8192]{0:T(1024)S(1)} %bitcast.56, f32[8192]{0:T(1024)S(1)} %bitcast.58, f32[8192]{0:T(1024)S(1)} %bitcast.60, f32[8192]{0:T(1024)S(1)} %bitcast.62, ...), kind=kLoop, calls=%fused_computation.1 | loop fusion | flops 7864320 | bytes 4456448 | tf_op jit(solution)/shard_map/add | solution.py:41
  22.2 0.1 fusion.66
  22.4 0.0 collective-permute-done
  22.4 0.5 fusion.23
  22.9 6.6 %slice_reduce_fusion.1 = (f32[2,16,8192]{2,1,0:T(8,128)}, f32[2,16,8192]{2,1,0:T(8,128)S(1)}) fusion(f32[2,2,16,8192]{3,1,2,0:T(2,128)S(1)} %fusion.23), kind=kLoop, calls=%fused_computation.27 | loop fusion | bytes 4194304 | tf_op jit(solution)/shard_map/slice | solution.py:58
  29.5 2.2 %reshape_squeeze.6 = f32[2,16,128,64]{3,2,1,0:T(8,128)S(1)} reshape(f32[2,16,8192]{2,1,0:T(8,128)} %get-tuple-element.17) | data formatting | bytes 2097152 | tf_op jit(solution)/shard_map/reshape;squeeze | solution.py:58
  31.7 4.4 %fusion.33 = f32[2,16,64,128]{3,2,1,0:T(8,128)} fusion(f32[2,16,128,64]{3,2,1,0:T(8,128)S(1)} %reshape_squeeze.6), kind=kOutput, calls=%fused_computation.59 | convolution fusion | flops 402882560 | bytes 2097152 | tf_op jit(solution)/shard_map/kn,pfnm->pfmk/dot_general | solution.py:30
  36.1 2.2 %reshape_squeeze.7 = f32[2,16,128,64]{3,2,1,0:T(8,128)} reshape(f32[2,16,8192]{2,1,0:T(8,128)S(1)} %get-tuple-element.18) | data formatting | bytes 2097152 | tf_op jit(solution)/shard_map/reshape;squeeze | solution.py:59
  38.3 0.0 copy-start
  38.3 0.0 copy-start.1
  38.3 5.2 %fusion.31 = f32[2,16,64,128]{3,2,1,0:T(8,128)S(1)} fusion(f32[2,16,128,64]{3,2,1,0:T(8,128)} %reshape_squeeze.7), kind=kOutput, calls=%fused_computation.57 | convolution fusion | flops 402882560 | bytes 2097152 | tf_op jit(solution)/shard_map/kn,pfnm->pfmk/dot_general | solution.py:30
  43.6 0.0 copy-done
  43.6 0.0 copy-done.1
  43.6 3.5 %convolution_subtract_fusion.1 = f32[2,16,64,128]{3,2,1,0:T(8,128)S(1)} fusion(f32[2,16,64,128]{3,2,1,0:T(8,128)S(1)} %copy-done.1, f32[2,16,128,64]{3,2,1,0:T(8,128)S(1)} %copy-done), kind=kOutput, calls=%fused_computation.23 | convolution fusion | flops 403144704 | bytes 3145728 | tf_op jit(solution)/shard_map/kn,pfnm->pfmk/dot_general | solution.py:30
  47.1 3.7 %convolution_add_fusion.1 = f32[2,16,64,128]{3,2,1,0:T(8,128)S(1)} fusion(f32[2,16,64,128]{3,2,1,0:T(8,128)S(1)} %fusion.31, f32[2,16,128,64]{3,2,1,0:T(8,128)S(1)} %reshape_squeeze.6), kind=kOutput, calls=%fused_computation.22 | convolution fusion | flops 403144704 | bytes 3145728 | tf_op jit(solution)/shard_map/kn,pfnm->pfmk/dot_general | solution.py:30
  50.8 1.3 fusion.25
  52.1 1.3 fusion.24
  53.4 1.4 fusion.8
  54.8 1.5 fusion.101
  56.3 0.7 copy.24
  57.0 0.0 all-reduce.4.cloned.1.call-update
  57.0 0.2 reshape.95
  57.2 126.8 %all-reduce.4.cloned.1.call-done = f32[2,8192]{1,0:T(2,128)} async-done(((f32[2,8192]{1,0:T(2,128)}), f32[2,8192]{1,0:T(2,128)}) %all-reduce.4.cloned.1.call-update) | async-done | bytes 65552 | tf_op jit(solution)/shard_map/psum | solution.py:75
  184.0 0.9 broadcast_multiply_fusion
  184.8 1.1 broadcast_subtract_fusion
  (1 shorter events, 0.0 us)
Async XLA Ops:
  6.5 177.4 %all-reduce.4.cloned.1.call-start = ((), (), s32[]{:S(2)}) async-start(), calls=%async_computation | async-start | bytes 131072 | tf_op jit(solution)/shard_map/psum | solution.py:75
  13.8 8.6 %collective-permute-start = (f32[2,2,7,8192]{3,1,2,0:T(2,128)S(1)}, f32[2,2,7,8192]{3,1,2,0:T(2,128)S(1)}, u32[]{:S(2)}, u32[]{:S(2)}) collective-permute-start(f32[2,2,7,8192]{3,1,2,0:T(2,128)S(1)} %multiply_add_fusion.2), channel_id=1, source_target_pairs={{1,0},{2,1},{3,2},{5,4},{6,5},{7,6},{9,8},{10,9},{11,10},{13,12},{... | collective-permute-start | bytes 2752520 | tf_op jit(solution)/shard_map/ppermute | solution.py:14
  38.3 5.2 %copy-start = (f32[2,16,128,64]{3,2,1,0:T(8,128)S(1)}, f32[2,16,128,64]{3,2,1,0:T(8,128)}, u32[]{:S(2)}) copy-start(f32[2,16,128,64]{3,2,1,0:T(8,128)} %reshape_squeeze.7) | copy-start | bytes 3145732
  38.3 5.2 %copy-start.1 = (f32[2,16,64,128]{3,2,1,0:T(8,128)S(1)}, f32[2,16,64,128]{3,2,1,0:T(8,128)}, u32[]{:S(2)}) copy-start(f32[2,16,64,128]{3,2,1,0:T(8,128)} %fusion.33) | copy-start | bytes 3145732
Sparse Core Ops, SparseCore 0:
  57.1 126.7 all-reduce.3
where the time goes:
time: 194 us; the launch traced here: 193 us
  waiting for transfers between devices  127 us (65%)
  matrix products  22.3 us (11%)
  local copies, waits for them, and re-layouts  17.4 us (9%)
  between operations  13.5 us (7%)
  other arithmetic  11.4 us (6%)
    psum x1, waiting for transfers between devices, body(): channel_sum = lax.psum(totals, ('beam', 'tm'))  127 us
    dot_general x8, matrix products, apply(): return jnp.einsum(form, table, values, precision=lax.Precision.HIGHEST)  22.3 us
    add x2, other arithmetic, tap_sum(): result + filter_taps[tap_index] * source[:, :, tap_index:tap_index + count]  8.76 us
    slice x1, local copies, waits for them, and re-layouts, body(): grid_real = filtered[:, 0].reshape(2, frames, RADIX, stride)  6.58 us
    unnamed x6, local copies, waits for them, and re-layouts  3.9 us
  transfers between devices with their start and end apart: 2, of which 1 were waited for; matrix products, arithmetic and copies ran while one was open for 4% of the time, Pallas kernels for 0%

commit v1 on v0

--- a/solution.py
+++ b/solution.py
@@ -1,8 +1,11 @@
+import functools
 import math
 
 import jax
 import jax.numpy as jnp
 from jax import lax
+from jax.experimental import pallas as pl
+from jax.experimental.pallas import tpu as pltpu
 from jax.sharding import PartitionSpec as P
 
 RADIX = 128
@@ -27,7 +30,7 @@
 def complex_apply(form, table_cos, table_sin, real_part, imag_part):
 
     def apply(table, values):
-        return jnp.einsum(form, table, values, precision=lax.Precision.HIGHEST)
+        return jnp.einsum(form, table, values, precision=lax.Precision.HIGH)
 
     return (
         apply(table_cos, real_part) - apply(table_sin, imag_part),
@@ -40,6 +43,92 @@
     for tap_index in range(1, filter_taps.shape[0]):
         result = result + filter_taps[tap_index] * source[:, :, tap_index : tap_index + count]
     return result
+
+
+def remote(src, dst, send, recv, beam, tm):
+    return pltpu.make_async_remote_copy(
+        src_ref=src, dst_ref=dst, send_sem=send, recv_sem=recv,
+        device_id=(beam, tm), device_id_type=pl.DeviceIdType.MESH,
+    )
+
+
+def greet(beams, tms):
+    b, t = lax.axis_index("beam"), lax.axis_index("tm")
+    barrier = pltpu.get_barrier_semaphore()
+    for d in range(1, tms):
+        pl.semaphore_signal(barrier, inc=1, device_id=(b, lax.rem(t + d, tms)), device_id_type=pl.DeviceIdType.MESH)
+    for d in range(1, beams):
+        pl.semaphore_signal(barrier, inc=1, device_id=(lax.rem(b + d, beams), t), device_id_type=pl.DeviceIdType.MESH)
+    pl.semaphore_wait(barrier, tms - 1 + beams - 1)
+
+
+def total_all(beams, tms, tot, res, part, whole, in_tm, in_beam, sems):
+    b, t = lax.axis_index("beam"), lax.axis_index("tm")
+    rows = tot.shape[0] // tms
+    s1, r1, s2, r2, s3, r3 = sems
+
+    def block(i):
+        return pl.ds(pl.multiple_of(i * rows, rows), rows)
+
+    copies = []
+    for d in range(1, tms):
+        peer = lax.rem(t + d, tms)
+        copies.append(remote(tot.at[block(peer)], in_tm.at[d - 1], s1.at[d - 1], r1.at[d - 1], b, peer))
+        copies[-1].start()
+    own = tot[block(t), :]
+    for d in range(1, tms):
+        copies[d - 1].wait_recv()
+        own = own + in_tm[d - 1]
+    part[...] = own
+    second = []
+    for d in range(1, beams):
+        peer = lax.rem(b + d, beams)
+        second.append(remote(part, in_beam.at[d - 1], s2.at[d - 1], r2.at[d - 1], peer, t))
+        second[-1].start()
+    for d in range(1, beams):
+        second[d - 1].wait_recv()
+        own = own + in_beam[d - 1]
+    whole[...] = own
+    third = []
+    for d in range(1, tms):
+        peer = lax.rem(t + d, tms)
+        third.append(remote(whole, res.at[block(t)], s3.at[d - 1], r3.at[d - 1], b, peer))
+        third[-1].start()
+    res[block(t), :] = own
+    for c in third:
+        c.wait_recv()
+    for c in copies + second + third:
+        c.wait_send()
+
+
+def total_scratch(beams, tms, rows):
+    share = (rows // tms, 128)
+    sem = pltpu.SemaphoreType.DMA
+    return [
+        pltpu.VMEM(share, jnp.float32),
+        pltpu.VMEM(share, jnp.float32),
+        pltpu.VMEM((tms - 1, *share), jnp.float32),
+        pltpu.VMEM((beams - 1, *share), jnp.float32),
+        sem((tms - 1,)), sem((tms - 1,)), sem((beams - 1,)), sem((beams - 1,)), sem((tms - 1,)), sem((tms - 1,)),
+    ]
+
+
+def total_kernel(beams, tms, tot, res, part, whole, in_tm, in_beam, *sems):
+    greet(beams, tms)
+    total_all(beams, tms, tot, res, part, whole, in_tm, in_beam, sems)
+
+
+def total_of_all(tot):
+    beams, tms = lax.axis_size("beam"), lax.axis_size("tm")
+    return pl.pallas_call(
+        functools.partial(total_kernel, beams, tms),
+        out_shape=jax.ShapeDtypeStruct(tot.shape, tot.dtype),
+        in_specs=[pl.BlockSpec(memory_space=pltpu.VMEM)],
+        out_specs=pl.BlockSpec(memory_space=pltpu.VMEM),
+        scratch_shapes=total_scratch(beams, tms, tot.shape[0]),
+        compiler_params=pltpu.CompilerParams(collective_id=0, has_side_effects=True),
+        name="total_of_all",
+    )(tot)
 
 
 def body(voltages, filter_taps):
@@ -72,7 +161,7 @@
         2, frames, channels
     )
     totals = jnp.sum(powers, axis=1)
-    channel_sum = lax.psum(totals, ("beam", "tm"))
+    channel_sum = total_of_all(totals.reshape(-1, 128)).reshape(totals.shape)
     all_frames = frames * lax.axis_size("tm")
     all_beams = voltages.shape[0] * lax.axis_size("beam")
     baseline = channel_sum / all_frames / all_beams

time: 194 us -> 66 us (0.34)
  waiting for transfers between devices: 127 us -> 0.01 us
  Pallas kernels: 0 us -> 22 us
  between operations: 13.5 us -> 0.16 us
  matrix products: 22.3 us -> 14 us
    psum x1 -> x0, waiting for transfers between devices: 127 us -> none  [body(): channel_sum = lax.psum(totals, ('beam', 'tm'))]
    pallas_call x0 -> x1, Pallas kernels: none -> 22 us  [total_of_all(): pl.pallas_call(functools.partial(total_kernel, beams, tms), out_shape=jax...]
    dot_general x8, matrix products: 22.3 us -> 14 us  [apply(): return jnp.einsum(form, table, values, precision=lax.Precision.HIGH)]
    unnamed x6 -> x5, local copies, waits for them, and re-layouts: 3.9 us -> 3.22 us
  transfers between devices with their start and end apart: 2 -> 1, of which waited for: 1 -> 0; matrix products, arithmetic and copies ran while one was open for 4% -> 11% of each run, Pallas kernels for 0% -> 0%
where the time goes in v1:
time: 66 us; the launch traced here: 65.7 us
  Pallas kernels  22 us (33%)
  local copies, waits for them, and re-layouts  17 us (26%)
  matrix products  14 us (21%)
  other arithmetic  11.4 us (17%)
  starting transfers between devices  1.29 us (2%)
    pallas_call x1, Pallas kernels, total_of_all(): pl.pallas_call(functools.partial(total_kernel, beams, tms), out_shape=jax...  22 us
    dot_general x8, matrix products, apply(): return jnp.einsum(form, table, values, precision=lax.Precision.HIGH)  14 us
    add x2, other arithmetic, tap_sum(): result + filter_taps[tap_index] * source[:, :, tap_index:tap_index + count]  8.76 us
    slice x1, local copies, waits for them, and re-layouts, body(): grid_real = filtered[:, 0].reshape(2, frames, RADIX, stride)  6.58 us
    unnamed x5, local copies, waits for them, and re-layouts  3.22 us
    slice x1, local copies, waits for them, and re-layouts, tap_sum(): result = filter_taps[0] * source[:, :, 0:count]  2.54 us
    another operation x1, local copies, waits for them, and re-layouts, body(): grid_imag = filtered[:, 1].reshape(2, frames, RADIX, stride)  2.19 us
    another operation x1, local copies, waits for them, and re-layouts, body(): grid_real = filtered[:, 0].reshape(2, frames, RADIX, stride)  2.18 us
  transfers between devices with their start and end apart: 1, of which 0 were waited for; matrix products, arithmetic and copies ran while one was open for 11% of the time, Pallas kernels for 0%

profile of v1, /device:TPU:0, one launch (start us, length us, event | category | flops | bytes accessed | tf_op | source)
XLA Modules:
  0.0 65.7 jit_solution(4214675853381554649)
XLA Ops:
  0.0 2.5 %fusion.100 = (f32[1,8192]{1,0:T(1,128)S(1)}, f32[1,8192]{1,0:T(1,128)S(1)}, f32[1,8192]{1,0:T(1,128)S(1)}, f32[1,8192]{1,0:T(1,128)S(1)}, f32[1,8192]{1,0:T(1,1...) fusion(f32[8,8192]{1,0:T(8,128)} %param.5), kind=kLoop, calls=%fused_computation.125 | loop fusion | bytes 524288 | tf_op jit(solution)/shard_map/slice | solution.py:42
  2.6 3.2 %copy.21 = f32[1,2,2,16,8192]{4,2,3,1,0:T(2,128)S(1)} copy(f32[1,2,2,16,8192]{4,3,2,1,0:T(8,128)} %param.4) | data formatting | bytes 4194304 | tf_op args[0]
  5.8 0.1 slice.135
  5.8 1.6 %multiply_add_fusion.2 = f32[2,2,7,8192]{3,1,2,0:T(2,128)S(1)} fusion(f32[2,2,7,8192]{3,1,2,0:T(2,128)S(1)} %slice.135, f32[8192]{0:T(1024)S(1)} %bitcast.62, f32[8192]{0:T(1024)S(1)} %bitcast.64, f32[8192]{0:T(1024)S(1)} %bitcast.52, f32[8192]{0:T(1024)S(1)} %bitcast.54, f32[8192]{0:T(1024)S(1)} %bitcast.56, f32[8192]{0:T(1024)S(1)} %bitcast.58, ...), kind=kLoop, calls=%fused_computation.44 | loop fusion | flops 3211264 | bytes 2097152 | tf_op jit(solution)/shard_map/add | solution.py:44
  7.4 1.3 %collective-permute-start = (f32[2,2,7,8192]{3,1,2,0:T(2,128)S(1)}, f32[2,2,7,8192]{3,1,2,0:T(2,128)S(1)}, u32[]{:S(2)}, u32[]{:S(2)}) collective-permute-start(f32[2,2,7,8192]{3,1,2,0:T(2,128)S(1)} %multiply_add_fusion.2), channel_id=1, source_target_pairs={{1,0},{2,1},{3,2},{5,4},{6,5},{7,6},{9,8},{10,9},{11,10},{13,12},{... | collective-permute-start | bytes 2752520 | tf_op jit(solution)/shard_map/ppermute | solution.py:17
  8.7 7.2 %multiply_add_fusion = f32[2,2,16,8192]{3,1,2,0:T(2,128)S(1)} fusion(f32[2,2,16,8192]{3,1,2,0:T(2,128)S(1)} %bitcast.51, f32[8192]{0:T(1024)S(1)} %bitcast.63, f32[8192]{0:T(1024)S(1)} %bitcast.65, f32[8192]{0:T(1024)S(1)} %bitcast.53, f32[8192]{0:T(1024)S(1)} %bitcast.55, f32[8192]{0:T(1024)S(1)} %bitcast.57, f32[8192]{0:T(1024)S(1)} %bitcast.59, ...), kind=kLoop, calls=%fused_computation.1 | loop fusion | flops 7864320 | bytes 4456448 | tf_op jit(solution)/shard_map/add | solution.py:44
  15.9 0.1 fusion.66
  16.1 0.0 collective-permute-done
  16.1 0.5 fusion.23
  16.6 6.6 %slice_reduce_fusion.1 = (f32[2,16,8192]{2,1,0:T(8,128)}, f32[2,16,8192]{2,1,0:T(8,128)S(1)}) fusion(f32[2,2,16,8192]{3,1,2,0:T(2,128)S(1)} %fusion.23), kind=kLoop, calls=%fused_computation.27 | loop fusion | bytes 4194304 | tf_op jit(solution)/shard_map/slice | solution.py:147
  23.2 2.2 %reshape_squeeze.6 = f32[2,16,128,64]{3,2,1,0:T(8,128)S(1)} reshape(f32[2,16,8192]{2,1,0:T(8,128)} %get-tuple-element.17) | data formatting | bytes 2097152 | tf_op jit(solution)/shard_map/reshape;squeeze | solution.py:147
  25.4 2.8 %fusion.33 = f32[2,16,64,128]{3,2,1,0:T(8,128)} fusion(f32[2,16,128,64]{3,2,1,0:T(8,128)S(1)} %reshape_squeeze.6), kind=kOutput, calls=%fused_computation.58 | convolution fusion | flops 201555968 | bytes 2097152 | tf_op jit(solution)/shard_map/kn,pfnm->pfmk/dot_general | solution.py:33
  28.2 2.2 %reshape_squeeze.7 = f32[2,16,128,64]{3,2,1,0:T(8,128)} reshape(f32[2,16,8192]{2,1,0:T(8,128)S(1)} %get-tuple-element.18) | data formatting | bytes 2097152 | tf_op jit(solution)/shard_map/reshape;squeeze | solution.py:148
  30.4 0.0 copy-start
  30.4 0.0 copy-start.1
  30.4 3.6 %fusion.31 = f32[2,16,64,128]{3,2,1,0:T(8,128)S(1)} fusion(f32[2,16,128,64]{3,2,1,0:T(8,128)} %reshape_squeeze.7), kind=kOutput, calls=%fused_computation.56 | convolution fusion | flops 201555968 | bytes 2097152 | tf_op jit(solution)/shard_map/kn,pfnm->pfmk/dot_general | solution.py:33
  34.0 0.0 copy-done
  34.0 0.0 copy-done.1
  34.0 1.8 %convolution_subtract_fusion.1 = f32[2,16,64,128]{3,2,1,0:T(8,128)S(1)} fusion(f32[2,16,64,128]{3,2,1,0:T(8,128)S(1)} %copy-done.1, f32[2,16,128,64]{3,2,1,0:T(8,128)S(1)} %copy-done), kind=kOutput, calls=%fused_computation.23 | convolution fusion | flops 201818112 | bytes 3145728 | tf_op jit(solution)/shard_map/kn,pfnm->pfmk/dot_general | solution.py:33
  35.9 1.9 %convolution_add_fusion.1 = f32[2,16,64,128]{3,2,1,0:T(8,128)S(1)} fusion(f32[2,16,64,128]{3,2,1,0:T(8,128)S(1)} %fusion.31, f32[2,16,128,64]{3,2,1,0:T(8,128)S(1)} %reshape_squeeze.6), kind=kOutput, calls=%fused_computation.22 | convolution fusion | flops 201818112 | bytes 3145728 | tf_op jit(solution)/shard_map/kn,pfnm->pfmk/dot_general | solution.py:33
  37.7 0.7 %fusion.25 = f32[2,16,128,64]{2,3,1,0:T(8,128)S(1)} fusion(f32[2,16,64,128]{3,2,1,0:T(8,128)S(1)} %convolution_add_fusion.1, f32[2,16,64,128]{3,2,1,0:T(8,128)S(1)} %convolution_subtract_fusion.1, f32[64,128]{1,0:T(8,128)S(1)} %get-tuple-element.29, f32[64,128]{1,0:T(8,128)S(1)} %get-tuple-element.30), kind=kOutput, calls=%fused_computation.47 | convolution fusion | flops 101507072 | bytes 3211264 | tf_op jit(solution)/shard_map/jm,pfmk->pfjk/dot_general | solution.py:33
  38.5 0.7 %fusion.24 = f32[2,16,128,64]{2,3,1,0:T(8,128)S(1)} fusion(f32[2,16,64,128]{3,2,1,0:T(8,128)S(1)} %convolution_add_fusion.1, f32[2,16,64,128]{3,2,1,0:T(8,128)S(1)} %convolution_subtract_fusion.1, f32[64,128]{1,0:T(8,128)S(1)} %get-tuple-element.29, f32[64,128]{1,0:T(8,128)S(1)} %get-tuple-element.30), kind=kOutput, calls=%fused_computation.46 | convolution fusion | flops 101507072 | bytes 3211264 | tf_op jit(solution)/shard_map/jm,pfmk->pfjk/dot_general | solution.py:33
  39.3 0.8 %fusion.8 = f32[2,16,128,64]{2,3,1,0:T(8,128)S(1)} fusion(f32[2,16,128,64]{2,3,1,0:T(8,128)S(1)} %fusion.24, f32[2,16,64,128]{3,2,1,0:T(8,128)S(1)} %convolution_add_fusion.1, f32[2,16,64,128]{3,2,1,0:T(8,128)S(1)} %convolution_subtract_fusion.1, f32[64,128]{1,0:T(8,128)S(1)} %get-tuple-element.29, f32[64,128]{1,0:T(8,128)S(1)} %get-tuple-element.30), kind=kOutput, calls=%fused_computation.21 | convolution fusion | flops 102031360 | bytes 4259840 | tf_op jit(solution)/shard_map/jm,pfmk->pfjk/dot_general | solution.py:33
  40.0 1.6 %fusion.101 = (f32[2,64,128]{2,1,0:T(8,128)}, f32[2,16,64,128]{3,2,1,0:T(8,128)S(1)}) fusion(f32[2,16,128,64]{2,3,1,0:T(8,128)S(1)} %fusion.8, f32[2,16,128,64]{2,3,1,0:T(8,128)S(1)} %fusion.25, f32[2,16,64,128]{3,2,1,0:T(8,128)S(1)} %convolution_add_fusion.1, f32[2,16,64,128]{3,2,1,0:T(8,128)S(1)} %convolution_subtract_fusion.1, ...), kind=kOutput, calls=%fused_computation.126 | convolution fusion | flops 102801408 | bytes 5373952 | tf_op jit(solution)/shard_map/jm,pfmk->pfjk/dot_general | solution.py:33
  41.6 0.2 reshape.106
  41.8 22.0 %total_of_all.1 = f32[128,128]{1,0:T(8,128)} custom-call(f32[128,128]{1,0:T(8,128)} %bitcast.68), custom_call_target="tpu_custom_call" | custom-call | tf_op jit(solution)/shard_map/total_of_all/pallas_call | solution.py:123
  63.8 0.8 %broadcast_multiply_fusion = f32[128,128]{1,0:T(8,128)S(1)} fusion(f32[128,128]{1,0:T(8,128)} %total_of_all.1), kind=kLoop, calls=%fused_computation.79 | loop fusion | flops 16384 | bytes 131072 | tf_op jit(solution)/shard_map/div | solution.py:167
  64.7 1.1 %broadcast_subtract_fusion = f32[1,2,16,8192]{3,2,1,0:T(8,128)} fusion(f32[1,2,16,8192]{3,2,1,0:T(8,128)S(1)} %reshape.106, f32[2,8192]{1,0:T(2,128)S(1)} %div.23), kind=kLoop, calls=%fused_computation.45 | loop fusion | flops 262144 | bytes 2162688 | tf_op jit(solution)/shard_map/sub | solution.py:168
  (2 shorter events, 0.0 us)
Async XLA Ops:
  7.4 8.6 %collective-permute-start = (f32[2,2,7,8192]{3,1,2,0:T(2,128)S(1)}, f32[2,2,7,8192]{3,1,2,0:T(2,128)S(1)}, u32[]{:S(2)}, u32[]{:S(2)}) collective-permute-start(f32[2,2,7,8192]{3,1,2,0:T(2,128)S(1)} %multiply_add_fusion.2), channel_id=1, source_target_pairs={{1,0},{2,1},{3,2},{5,4},{6,5},{7,6},{9,8},{10,9},{11,10},{13,12},{... | collective-permute-start | bytes 2752520 | tf_op jit(solution)/shard_map/ppermute | solution.py:17
  30.4 3.6 %copy-start = (f32[2,16,128,64]{3,2,1,0:T(8,128)S(1)}, f32[2,16,128,64]{3,2,1,0:T(8,128)}, u32[]{:S(2)}) copy-start(f32[2,16,128,64]{3,2,1,0:T(8,128)} %reshape_squeeze.7) | copy-start | bytes 3145732
  30.4 3.6 %copy-start.1 = (f32[2,16,64,128]{3,2,1,0:T(8,128)S(1)}, f32[2,16,64,128]{3,2,1,0:T(8,128)}, u32[]{:S(2)}) copy-start(f32[2,16,64,128]{3,2,1,0:T(8,128)} %fusion.33) | copy-start | bytes 3145732

commit v2 on v1

--- a/solution.py
+++ b/solution.py
@@ -3,46 +3,20 @@
 
 import jax
 import jax.numpy as jnp
+import numpy as np
 from jax import lax
 from jax.experimental import pallas as pl
 from jax.experimental.pallas import tpu as pltpu
 from jax.sharding import PartitionSpec as P
 
-RADIX = 128
+LANES = 128
+GROUP = 8
 
 
 def passed_along(x, axis, by):
     devices = lax.axis_size(axis)
     pairs = [(i, i + by) for i in range(devices) if 0 <= i + by < devices]
     return lax.ppermute(x, axis, pairs)
-
-
-def twiddles(rows_count, cols_count, modulus):
-    product = (
-        jnp.arange(rows_count, dtype=jnp.int32)[:, None]
-        * jnp.arange(cols_count, dtype=jnp.int32)[None, :]
-        % modulus
-    )
-    angles = product.astype(jnp.float32) * (-2.0 * math.pi / modulus)
-    return (jnp.cos(angles), jnp.sin(angles))
-
-
-def complex_apply(form, table_cos, table_sin, real_part, imag_part):
-
-    def apply(table, values):
-        return jnp.einsum(form, table, values, precision=lax.Precision.HIGH)
-
-    return (
-        apply(table_cos, real_part) - apply(table_sin, imag_part),
-        apply(table_cos, imag_part) + apply(table_sin, real_part),
-    )
-
-
-def tap_sum(filter_taps, source, count):
-    result = filter_taps[0] * source[:, :, 0:count]
-    for tap_index in range(1, filter_taps.shape[0]):
-        result = result + filter_taps[tap_index] * source[:, :, tap_index : tap_index + count]
-    return result
 
 
 def remote(src, dst, send, recv, beam, tm):
@@ -131,41 +105,239 @@
     )(tot)
 
 
+def tables(channels):
+    tiles = channels // LANES
+    angle = 2.0 * math.pi * (np.outer(np.arange(tiles), np.arange(LANES)) % channels) / channels
+    scale = channels ** -0.5
+    k2 = np.concatenate([np.arange(0, LANES, 2), np.arange(1, LANES, 2)])
+    last = 2.0 * math.pi * (np.outer(np.arange(LANES), k2) % LANES) / LANES
+    c, s = np.cos(last), np.sin(last)
+    matrix = jnp.asarray(np.block([[c, -s], [s, c]]).astype(np.float32))
+    high = matrix.astype(jnp.bfloat16)
+    low = (matrix - high.astype(jnp.float32)).astype(jnp.bfloat16)
+    return (
+        jnp.asarray((scale * np.cos(angle)).astype(np.float32)),
+        jnp.asarray((-scale * np.sin(angle)).astype(np.float32)),
+        high,
+        low,
+    )
+
+
+def times(x, turn, of):
+    turn = turn % of
+    re, im = x
+    if turn == 0:
+        return x
+    if 4 * turn == of:
+        return im, -re
+    if 2 * turn == of:
+        return -re, -im
+    if 4 * turn == 3 * of:
+        return -im, re
+    c, s = math.cos(2 * math.pi * turn / of), math.sin(2 * math.pi * turn / of)
+    if 8 * turn % of == 0:
+        h = abs(c)
+        if 8 * turn == of:
+            return (re + im) * h, (im - re) * h
+        if 8 * turn == 3 * of:
+            return (im - re) * h, (re + im) * -h
+    return re * c + im * s, im * c - re * s
+
+
+def add(x, y):
+    return x[0] + y[0], x[1] + y[1]
+
+
+def sub(x, y):
+    return x[0] - y[0], x[1] - y[1]
+
+
+def transform(xs):
+    n = len(xs)
+    if n == 1:
+        return xs
+    even, odd = transform(xs[0::2]), transform(xs[1::2])
+    odd = [times(o, k, n) for k, o in enumerate(odd)]
+    return [add(e, o) for e, o in zip(even, odd)] + [sub(e, o) for e, o in zip(even, odd)]
+
+
+def channelize(lo, hi, taps, tw_re, tw_im, high, low, xs, mid, rows_h, rows_l, pw, turned):
+    tap_count, channels = taps.shape
+    tiles = channels // LANES
+    outer = 8
+    inner = tiles // outer
+
+    def first(b, carry):
+        tiles_out = []
+        for a in range(outer):
+            cols = pl.ds(pl.multiple_of((a * inner + b) * LANES, LANES), LANES)
+            weights = taps[:, cols]
+            pair = []
+            for q in range(2):
+                base = (a * 2 + q) * 2 * GROUP
+                xs[base : base + GROUP, :] = lo[q, :, cols]
+                xs[base + GROUP : base + 2 * GROUP, :] = hi[q, :, cols]
+                total = weights[0:1] * lo[q, :, cols]
+                for t in range(1, tap_count):
+                    total = total + weights[t : t + 1] * xs[base + t : base + t + GROUP, :]
+                pair.append(total)
+            tiles_out.append(tuple(pair))
+        for c, z in enumerate(transform(tiles_out)):
+            at = pl.ds(pl.multiple_of((c * inner + b) * GROUP, GROUP), GROUP)
+            mid[0, at, :] = z[0]
+            mid[1, at, :] = z[1]
+        return carry
+
+    lax.fori_loop(0, inner, first, 0)
+
+    for c0 in range(0, outer, 2):
+        both = []
+        for c in (c0, c0 + 1):
+            zs = []
+            for b in range(inner):
+                at = slice((c * inner + b) * GROUP, (c * inner + b + 1) * GROUP)
+                zs.append(times((mid[0, at, :], mid[1, at, :]), b * c, tiles))
+            turned_out = []
+            for d, (re, im) in enumerate(transform(zs)):
+                k1 = c + outer * d
+                wr, wi = tw_re[k1 : k1 + 1, :], tw_im[k1 : k1 + 1, :]
+                turned_out.append((re * wr - im * wi, re * wi + im * wr))
+            both.append(turned_out)
+        for d in range(inner):
+            at = slice((c0 + outer * d) * GROUP, (c0 + outer * d + 2) * GROUP)
+            for q in range(2):
+                x = jnp.concatenate([both[0][d][q], both[1][d][q]], axis=0)
+                h = x.astype(jnp.bfloat16)
+                rows_h[at, q * LANES : (q + 1) * LANES] = h
+                rows_l[at, q * LANES : (q + 1) * LANES] = (x - h.astype(jnp.float32)).astype(jnp.bfloat16)
+
+    def dot(x, y):
+        return jnp.dot(x, y, preferred_element_type=jnp.float32)
+
+    spec = dot(rows_h[...], high[...]) + dot(rows_l[...], high[...]) + dot(rows_h[...], low[...])
+    spec_re, spec_im = spec[:, :LANES], spec[:, LANES:]
+    pw[...] = spec_re * spec_re + spec_im * spec_im
+
+    left = lax.broadcasted_iota(jnp.int32, (tiles, LANES), 1) < tiles
+    total = jnp.zeros((tiles, LANES), jnp.float32)
+    for f in range(0, GROUP, 2):
+        pair = jnp.concatenate(
+            [pw[pl.ds(f, tiles, stride=GROUP), :], pw[pl.ds(f + 1, tiles, stride=GROUP), :]], axis=0
+        ).T
+        upper, lower = pair[:tiles], pair[tiles:]
+        one = jnp.where(left, upper, pltpu.roll(lower, tiles, 1))
+        two = jnp.where(left, pltpu.roll(upper, tiles, 1), lower)
+        total = total + one + two
+        turned[pl.ds(f, tiles, stride=GROUP), :] = one
+        turned[pl.ds(f + 1, tiles, stride=GROUP), :] = two
+    return total
+
+
+def power_kernel(lo, hi, taps, tw_re, tw_im, high, low, so_far, *rest):
+    powers, total, *scratch = rest[-8:]
+    turned = scratch[-1]
+    part = channelize(lo.at[0], hi.at[0], taps, tw_re, tw_im, high, low, *scratch)
+    first = pl.program_id(1) == 0
+
+    @pl.when(first)
+    def _():
+        total[0] = so_far[0] + part
+
+    @pl.when(jnp.logical_not(first))
+    def _():
+        total[0] = total[0] + part
+
+    for j in range(part.shape[0]):
+        powers[0, :, j * LANES : (j + 1) * LANES] = turned[j * GROUP : (j + 1) * GROUP, :]
+
+
+def powers_of(lo, lo_at, hi, hi_at, taps, consts, so_far, powers, grid, out_at):
+    channels = taps.shape[1]
+    tiles = channels // LANES
+    rows = tiles * GROUP
+    block = (1, 2, GROUP, channels)
+    whole = pl.BlockSpec(memory_space=pltpu.VMEM)
+    total_spec = pl.BlockSpec((1, tiles, LANES), lambda p, g: (out_at(p, g)[0], 0, 0))
+    earlier = [] if powers is None else [powers]
+    return pl.pallas_call(
+        power_kernel,
+        grid=grid,
+        out_shape=(
+            jax.ShapeDtypeStruct((lo.shape[0], lo.shape[2], channels), jnp.float32),
+            jax.ShapeDtypeStruct(so_far.shape, so_far.dtype),
+        ),
+        in_specs=[
+            pl.BlockSpec(block, lo_at),
+            pl.BlockSpec(block, hi_at),
+            whole, whole, whole, whole, whole,
+            total_spec,
+        ]
+        + [pl.BlockSpec(memory_space=pl.ANY) for _ in earlier],
+        out_specs=(
+            pl.BlockSpec((1, GROUP, channels), lambda p, g: (*out_at(p, g), 0)),
+            total_spec,
+        ),
+        scratch_shapes=[
+            pltpu.VMEM((8 * 2 * 2 * GROUP, LANES), jnp.float32),
+            pltpu.VMEM((2, rows, LANES), jnp.float32),
+            pltpu.VMEM((rows, 2 * LANES), jnp.bfloat16),
+            pltpu.VMEM((rows, 2 * LANES), jnp.bfloat16),
+            pltpu.VMEM((rows, LANES), jnp.float32),
+            pltpu.VMEM((rows, LANES), jnp.float32),
+        ],
+        input_output_aliases={7: 1, 8: 0} if earlier else {7: 1},
+        cost_estimate=pl.CostEstimate(
+            flops=grid[0] * grid[1] * 1200 * 1000 * 1000,
+            bytes_accessed=grid[0] * grid[1] * 5 * GROUP * channels * 4,
+            transcendentals=0,
+        ),
+        name="powers_of",
+    )(lo, hi, taps, *consts, so_far, *earlier)
+
+
+def remove_kernel(scale, powers, sums, out):
+    for j in range(sums.shape[0]):
+        at = slice(j * LANES, (j + 1) * LANES)
+        out[0, 0, :, at] = powers[0, :, at] - sums[j : j + 1, :] * scale
+
+
+def removed(powers, sums, scale):
+    pols, frames, channels = powers.shape
+    tiles = channels // LANES
+    return pl.pallas_call(
+        functools.partial(remove_kernel, scale),
+        grid=(pols, frames // GROUP),
+        out_shape=jax.ShapeDtypeStruct((1, *powers.shape), powers.dtype),
+        in_specs=[
+            pl.BlockSpec((1, GROUP, channels), lambda p, g: (p, g, 0)),
+            pl.BlockSpec((tiles, LANES), lambda p, g: (p, 0)),
+        ],
+        out_specs=pl.BlockSpec((1, 1, GROUP, channels), lambda p, g: (0, p, g, 0)),
+        name="removed",
+    )(powers, sums)
+
+
 def body(voltages, filter_taps):
     segment = voltages[0]
-    frames = segment.shape[2]
-    channels = segment.shape[3]
-    rim_frames = filter_taps.shape[0] - 1
-    zero_rim = jnp.zeros((2, 2, rim_frames, channels), jnp.float32)
-    padded = jnp.concatenate([segment, zero_rim], axis=2)
-    filtered = tap_sum(filter_taps, padded, frames)
-    leading_rows = jnp.concatenate([zero_rim, segment[:, :, :rim_frames]], axis=2)
-    partial_value = tap_sum(filter_taps, leading_rows, rim_frames)
-    incoming = passed_along(partial_value, "tm", -1)
-    filtered = filtered.at[:, :, frames - rim_frames :].add(incoming)
-    stride = channels // RADIX
-    grid_real = filtered[:, 0].reshape(2, frames, RADIX, stride)
-    grid_imag = filtered[:, 1].reshape(2, frames, RADIX, stride)
-    cos_first, sin_first = twiddles(RADIX, RADIX, RADIX)
-    section_real, section_imag = complex_apply(
-        "kn,pfnm->pfmk", cos_first, sin_first, grid_real, grid_imag
+    pols, _, frames, channels = segment.shape
+    groups = frames // GROUP
+    tiles = channels // LANES
+    consts = tables(channels)
+    rims = [passed_along(segment[p : p + 1, :, :GROUP], "tm", -1) for p in range(pols)]
+    total = jnp.zeros((pols, tiles, LANES), jnp.float32)
+    powers, total = powers_of(
+        segment, lambda p, g: (p, 0, g, 0), segment, lambda p, g: (p, 0, g + 1, 0),
+        filter_taps, consts, total, None, (pols, groups - 1), lambda p, g: (p, g),
     )
-    twist_cos, twist_sin = twiddles(stride, RADIX, channels)
-    twisted_real = section_real * twist_cos - section_imag * twist_sin
-    twisted_imag = section_real * twist_sin + section_imag * twist_cos
-    cos_second, sin_second = twiddles(stride, stride, stride)
-    spec_real, spec_imag = complex_apply(
-        "jm,pfmk->pfjk", cos_second, sin_second, twisted_real, twisted_imag
-    )
-    powers = ((spec_real * spec_real + spec_imag * spec_imag) / channels).reshape(
-        2, frames, channels
-    )
-    totals = jnp.sum(powers, axis=1)
-    channel_sum = total_of_all(totals.reshape(-1, 128)).reshape(totals.shape)
+    for p in range(pols):
+        powers, total = powers_of(
+            segment, lambda _, g, p=p: (p, 0, groups - 1, 0), rims[p], lambda _, g: (0, 0, 0, 0),
+            filter_taps, consts, total, powers, (1, 1), lambda _, g, p=p: (p, groups - 1),
+        )
+    sums = total_of_all(total.reshape(pols * tiles, LANES))
     all_frames = frames * lax.axis_size("tm")
     all_beams = voltages.shape[0] * lax.axis_size("beam")
-    baseline = channel_sum / all_frames / all_beams
-    return (powers - baseline[:, None, :])[None]
+    return removed(powers, sums, 1.0 / (all_frames * all_beams))
 
 
 def solution(mesh):

time: 66 us -> 41.2 us (0.62)
  matrix products: 14 us -> 0 us
  local copies, waits for them, and re-layouts: 17 us -> 3.47 us
  Pallas kernels: 22 us -> 34.8 us
  other arithmetic: 11.4 us -> 0 us
  starting transfers between devices: 1.29 us -> 2.58 us
    pallas_call x0 -> x4, Pallas kernels: none -> 16 us  [the longest x3 12.5 us: powers_of(): pl.pallas_call(power_kernel, grid=grid, out_shape=(jax.ShapeDtypeStruct((...]
    dot_general x8 -> x0, matrix products: 14 us -> none  [apply(): return jnp.einsum(form, table, values, precision=lax.Precision.HIGH)]
    add x2 -> x0, other arithmetic: 8.76 us -> none  [tap_sum(): result + filter_taps[tap_index] * source[:, :, tap_index:tap_index + count]]
    slice x3 -> x1, local copies, waits for them, and re-layouts: 9.18 us -> 1.27 us  [body(): segment[p:p + 1, :, :GROUP]]
    another operation x2 -> x0, local copies, waits for them, and re-layouts: 4.37 us -> none  [the longest x1 2.19 us: body(): grid_imag = filtered[:, 1].reshape(2, frames, RADIX, stride)]
    pallas_call x1, Pallas kernels: 22 us -> 18.8 us  [total_of_all(): pl.pallas_call(functools.partial(total_kernel, beams, tms), out_shape=jax...]
    unnamed x5 -> x4, local copies, waits for them, and re-layouts: 3.22 us -> 1.58 us
    ppermute x1 -> x2, starting transfers between devices: 1.29 us -> 2.58 us  [passed_along(): return lax.ppermute(x, axis, pairs)]
  transfers between devices with their start and end apart: 1 -> 2, of which waited for: 0 -> 0; matrix products, arithmetic and copies ran while one was open for 11% -> 2% of each run, Pallas kernels for 0% -> 22%
where the time goes in v2:
time: 41.2 us; the launch traced here: 40.9 us
  Pallas kernels  34.8 us (84%)
  local copies, waits for them, and re-layouts  3.47 us (8%)
  starting transfers between devices  2.58 us (6%)
    pallas_call x1, Pallas kernels, total_of_all(): pl.pallas_call(functools.partial(total_kernel, beams, tms), out_shape=jax...  18.8 us
    pallas_call x3, Pallas kernels, powers_of(): pl.pallas_call(power_kernel, grid=grid, out_shape=(jax.ShapeDtypeStruct((...  12.5 us
    pallas_call x1, Pallas kernels, removed(): pl.pallas_call(functools.partial(remove_kernel, scale), grid=(pols, frame...  3.43 us
    ppermute x2, starting transfers between devices, passed_along(): return lax.ppermute(x, axis, pairs)  2.58 us
    unnamed x4, local copies, waits for them, and re-layouts  1.58 us
    slice x1, local copies, waits for them, and re-layouts, body(): segment[p:p + 1, :, :GROUP]  1.27 us
  transfers between devices with their start and end apart: 2, of which 0 were waited for; matrix products, arithmetic and copies ran while one was open for 2% of the time, Pallas kernels for 22%

profile of v2, /device:TPU:0, one launch (start us, length us, event | category | flops | bytes accessed | tf_op | source)
XLA Modules:
  0.0 40.9 jit_solution(11277341763544768849)
XLA Ops:
  0.0 1.3 %fusion = (f32[1,2,8,8192]{3,2,1,0:T(8,128)S(1)}, f32[1,2,8,8192]{3,2,1,0:T(8,128)S(1)}) fusion(f32[2,2,16,8192]{3,2,1,0:T(8,128)} %bitcast.2), kind=kLoop, calls=%fused_computation | loop fusion | bytes 2097152 | tf_op jit(solution)/shard_map/slice | solution.py:326
  1.3 1.3 %collective-permute-start.1 = (f32[1,2,8,8192]{3,2,1,0:T(8,128)S(1)}, f32[1,2,8,8192]{3,2,1,0:T(8,128)S(1)}, u32[]{:S(2)}, u32[]{:S(2)}) collective-permute-start(f32[1,2,8,8192]{3,2,1,0:T(8,128)S(1)} %get-tuple-element.17), channel_id=1, source_target_pairs={{1,0},{2,1},{3,2},{5,4},{6,5},{7,6},{9,8},{10,9},{11,10},{13,12},{... | collective-permute-start | bytes 1572872 | tf_op jit(solution)/shard_map/ppermute | solution.py:19
  2.6 1.3 %collective-permute-start = (f32[1,2,8,8192]{3,2,1,0:T(8,128)S(1)}, f32[1,2,8,8192]{3,2,1,0:T(8,128)S(1)}, u32[]{:S(2)}, u32[]{:S(2)}) collective-permute-start(f32[1,2,8,8192]{3,2,1,0:T(8,128)S(1)} %get-tuple-element.18), channel_id=1, source_target_pairs={{1,0},{2,1},{3,2},{5,4},{6,5},{7,6},{9,8},{10,9},{11,10},{13,12},{... | collective-permute-start | bytes 1572872 | tf_op jit(solution)/shard_map/ppermute | solution.py:19
  3.9 0.6 %broadcast_in_dim.3.so_far = f32[2,64,128]{2,1,0:T(8,128)} broadcast(f32[]{:T(128)} %constant.3.clone.1), dimensions={} | broadcast | bytes 65540 | tf_op jit(solution)/shard_map/broadcast_in_dim | solution.py:327
  4.5 5.3 %powers_of.3 = (f32[2,16,8192]{2,1,0:T(8,128)}, f32[2,64,128]{2,1,0:T(8,128)}) custom-call(f32[2,2,16,8192]{3,2,1,0:T(8,128)} %bitcast.3, f32[2,2,16,8192]{3,2,1,0:T(8,128)} %bitcast.4, f32[8,8192]{1,0:T(8,128)} %taps.5, f32[64,128]{1,0:T(8,128)} %constant.9.clone.tw_re, f32[64,128]{1,0:T(8,128)} %constant.10.clone.tw_im, ...), custom_call_target="tpu_custom_call", output_to_operand_aliasing={{1}: (7, {})} | custom-call | flops 2400000000 | bytes 2621440 | tf_op jit(solution)/shard_map/powers_of/pallas_call | solution.py:262
  9.8 0.0 collective-permute-done.1.hi
  9.9 0.0 copy-start.1
  9.9 0.8 %copy-done.1 = f32[1,2,8,8192]{3,2,1,0:T(8,128)} copy-done((f32[1,2,8,8192]{3,2,1,0:T(8,128)}, f32[1,2,8,8192]{3,2,1,0:T(8,128)S(1)}, u32[]{:S(2)}) %copy-start.1) | copy-done | bytes 524312
  10.7 3.6 %powers_of.4 = (f32[2,16,8192]{2,1,0:T(8,128)}, f32[2,64,128]{2,1,0:T(8,128)}) custom-call(f32[2,2,16,8192]{3,2,1,0:T(8,128)} %bitcast.5, f32[1,2,8,8192]{3,2,1,0:T(8,128)} %copy-done.1, f32[8,8192]{1,0:T(8,128)} %taps.5, f32[64,128]{1,0:T(8,128)} %constant.9.clone.tw_re, ...), custom_call_target="tpu_custom_call", output_to_operand_aliasing={{1}: (7, {}), {0}: (8, {})} | custom-call | flops 1200000000 | bytes 1310720 | tf_op jit(solution)/shard_map/powers_of/pallas_call | solution.py:262
  14.3 0.0 collective-permute-done.hi
  14.3 0.0 copy-start
  14.3 0.8 %copy-done = f32[1,2,8,8192]{3,2,1,0:T(8,128)} copy-done((f32[1,2,8,8192]{3,2,1,0:T(8,128)}, f32[1,2,8,8192]{3,2,1,0:T(8,128)S(1)}, u32[]{:S(2)}) %copy-start) | copy-done | bytes 524312
  15.1 3.6 %powers_of.5 = (f32[2,16,8192]{2,1,0:T(8,128)}, f32[2,64,128]{2,1,0:T(8,128)}) custom-call(f32[2,2,16,8192]{3,2,1,0:T(8,128)} %bitcast.6, f32[1,2,8,8192]{3,2,1,0:T(8,128)} %copy-done, f32[8,8192]{1,0:T(8,128)} %taps.5, f32[64,128]{1,0:T(8,128)} %constant.9.clone.tw_re, ...), custom_call_target="tpu_custom_call", output_to_operand_aliasing={{1}: (7, {}), {0}: (8, {})} | custom-call | flops 1200000000 | bytes 1310720 | tf_op jit(solution)/shard_map/powers_of/pallas_call | solution.py:262
  18.7 18.8 %total_of_all.1.sums = f32[128,128]{1,0:T(8,128)} custom-call(f32[128,128]{1,0:T(8,128)} %bitcast.7), custom_call_target="tpu_custom_call" | custom-call | tf_op jit(solution)/shard_map/total_of_all/pallas_call | solution.py:97
  37.5 3.4 %removed.1 = f32[1,2,16,8192]{3,2,1,0:T(8,128)} custom-call(f32[2,16,8192]{2,1,0:T(8,128)} %get-tuple-element.15.powers, f32[128,128]{1,0:T(8,128)} %total_of_all.1.sums), custom_call_target="tpu_custom_call" | custom-call | tf_op jit(solution)/shard_map/removed/pallas_call | solution.py:307
Async XLA Ops:
  1.3 8.6 %collective-permute-start.1 = (f32[1,2,8,8192]{3,2,1,0:T(8,128)S(1)}, f32[1,2,8,8192]{3,2,1,0:T(8,128)S(1)}, u32[]{:S(2)}, u32[]{:S(2)}) collective-permute-start(f32[1,2,8,8192]{3,2,1,0:T(8,128)S(1)} %get-tuple-element.17), channel_id=1, source_target_pairs={{1,0},{2,1},{3,2},{5,4},{6,5},{7,6},{9,8},{10,9},{11,10},{13,12},{... | collective-permute-start | bytes 1572872 | tf_op jit(solution)/shard_map/ppermute | solution.py:19
  2.6 11.7 %collective-permute-start = (f32[1,2,8,8192]{3,2,1,0:T(8,128)S(1)}, f32[1,2,8,8192]{3,2,1,0:T(8,128)S(1)}, u32[]{:S(2)}, u32[]{:S(2)}) collective-permute-start(f32[1,2,8,8192]{3,2,1,0:T(8,128)S(1)} %get-tuple-element.18), channel_id=1, source_target_pairs={{1,0},{2,1},{3,2},{5,4},{6,5},{7,6},{9,8},{10,9},{11,10},{13,12},{... | collective-permute-start | bytes 1572872 | tf_op jit(solution)/shard_map/ppermute | solution.py:19
  9.9 0.8 %copy-start.1 = (f32[1,2,8,8192]{3,2,1,0:T(8,128)}, f32[1,2,8,8192]{3,2,1,0:T(8,128)S(1)}, u32[]{:S(2)}) copy-start(f32[1,2,8,8192]{3,2,1,0:T(8,128)S(1)} %collective-permute-done.1.hi) | copy-start | bytes 1572868
  14.3 0.8 %copy-start = (f32[1,2,8,8192]{3,2,1,0:T(8,128)}, f32[1,2,8,8192]{3,2,1,0:T(8,128)S(1)}, u32[]{:S(2)}) copy-start(f32[1,2,8,8192]{3,2,1,0:T(8,128)S(1)} %collective-permute-done.hi) | copy-start | bytes 1572868

commit v3 on v2

v3 whole, which is shorter than its diff:
```python
import functools
import math

import jax
import jax.numpy as jnp
import numpy as np
from jax import lax
from jax.experimental import pallas as pl
from jax.experimental.pallas import tpu as pltpu
from jax.sharding import PartitionSpec as P

LANES = 128
GROUP = 8


def remote(src, dst, send, recv, beam, tm):
    return pltpu.make_async_remote_copy(
        src_ref=src, dst_ref=dst, send_sem=send, recv_sem=recv,
        device_id=(beam, tm), device_id_type=pl.DeviceIdType.MESH,
    )


def greet(beams, tms):
    b, t = lax.axis_index("beam"), lax.axis_index("tm")
    barrier = pltpu.get_barrier_semaphore()
    for d in range(1, tms):
        pl.semaphore_signal(barrier, inc=1, device_id=(b, lax.rem(t + d, tms)), device_id_type=pl.DeviceIdType.MESH)
    for d in range(1, beams):
        pl.semaphore_signal(barrier, inc=1, device_id=(lax.rem(b + d, beams), t), device_id_type=pl.DeviceIdType.MESH)
    pl.semaphore_wait(barrier, tms - 1 + beams - 1)


class Total:
    def __init__(self, beams, tms, tot, res, first_row, count, part, whole, in_tm, in_beam, sems):
        self.beams, self.tms, self.tot, self.res = beams, tms, tot, res
        self.first_row, self.rows = first_row, count // tms
        self.part, self.whole, self.in_tm, self.in_beam, self.sems = part, whole, in_tm, in_beam, sems
        self.b, self.t = lax.axis_index("beam"), lax.axis_index("tm")
        self.sent = []

    def block(self, i):
        return pl.ds(pl.multiple_of(self.first_row + i * self.rows, self.rows), self.rows)

    def to_tm(self):
        s1, r1 = self.sems[:2]
        self.first = []
        for d in range(1, self.tms):
            peer = lax.rem(self.t + d, self.tms)
            self.first.append(remote(
                self.tot.at[self.block(peer)], self.in_tm.at[d - 1], s1.at[d - 1], r1.at[d - 1], self.b, peer))
            self.first[-1].start()

    def to_beams(self):
        s2, r2 = self.sems[2:4]
        own = self.tot[self.block(self.t), :]
        for d, copy in enumerate(self.first):
            copy.wait_recv()
            own = own + self.in_tm[d]
        self.part[...] = own
        self.second = []
        for d in range(1, self.beams):
            peer = lax.rem(self.b + d, self.beams)
            self.second.append(remote(
                self.part, self.in_beam.at[d - 1], s2.at[d - 1], r2.at[d - 1], peer, self.t))
            self.second[-1].start()

    def back(self):
        s3, r3 = self.sems[4:]
        own = self.part[...]
        for d, copy in enumerate(self.second):
            copy.wait_recv()
            own = own + self.in_beam[d]
        self.whole[...] = own
        self.third = []
        for d in range(1, self.tms):
            peer = lax.rem(self.t + d, self.tms)
            self.third.append(remote(
                self.whole, self.res.at[self.block(self.t)], s3.at[d - 1], r3.at[d - 1], self.b, peer))
            self.third[-1].start()
        self.res[self.block(self.t), :] = own

    def arrive(self):
        for copy in self.third:
            copy.wait_recv()

    def leave(self):
        for copy in self.first + self.second + self.third:
            copy.wait_send()


def total_scratch(beams, tms, rows):
    share = (rows // tms, LANES)
    sem = pltpu.SemaphoreType.DMA
    return [
        pltpu.VMEM(share, jnp.float32),
        pltpu.VMEM(share, jnp.float32),
        pltpu.VMEM((tms - 1, *share), jnp.float32),
        pltpu.VMEM((beams - 1, *share), jnp.float32),
        sem((tms - 1,)), sem((tms - 1,)), sem((beams - 1,)), sem((beams - 1,)), sem((tms - 1,)), sem((tms - 1,)),
    ]


TOTAL_SCRATCH = 10


def tables(channels):
    tiles = channels // LANES
    angle = 2.0 * math.pi * (np.outer(np.arange(tiles), np.arange(LANES)) % channels) / channels
    scale = channels ** -0.5
    k2 = np.concatenate([np.arange(0, LANES, 2), np.arange(1, LANES, 2)])
    last = 2.0 * math.pi * (np.outer(np.arange(LANES), k2) % LANES) / LANES
    c, s = np.cos(last), np.sin(last)
    matrix = jnp.asarray(np.block([[c, -s], [s, c]]).astype(np.float32))
    high = matrix.astype(jnp.bfloat16)
    low = (matrix - high.astype(jnp.float32)).astype(jnp.bfloat16)
    return (
        jnp.asarray((scale * np.cos(angle)).astype(np.float32)),
        jnp.asarray((-scale * np.sin(angle)).astype(np.float32)),
        high,
        low,
    )


def times(x, turn, of):
    turn = turn % of
    re, im = x
    if turn == 0:
        return x
    if 4 * turn == of:
        return im, -re
    if 2 * turn == of:
        return -re, -im
    if 4 * turn == 3 * of:
        return -im, re
    c, s = math.cos(2 * math.pi * turn / of), math.sin(2 * math.pi * turn / of)
    if 8 * turn % of == 0:
        h = abs(c)
        if 8 * turn == of:
            return (re + im) * h, (im - re) * h
        if 8 * turn == 3 * of:
            return (im - re) * h, (re + im) * -h
    return re * c + im * s, im * c - re * s


def add(x, y):
    return x[0] + y[0], x[1] + y[1]


def sub(x, y):
    return x[0] - y[0], x[1] - y[1]


def transform(xs):
    n = len(xs)
    if n == 1:
        return xs
    even, odd = transform(xs[0::2]), transform(xs[1::2])
    odd = [times(o, k, n) for k, o in enumerate(odd)]
    return [add(e, o) for e, o in zip(even, odd)] + [sub(e, o) for e, o in zip(even, odd)]


def channelize(lo, hi, taps, tw_re, tw_im, high, low, xs, mid, rows_h, rows_l, pw, turned):
    tap_count, channels = taps.shape
    tiles = channels // LANES
    outer = 8
    inner = tiles // outer

    def first(b, carry):
        tiles_out = []
        for a in range(outer):
            cols = pl.ds(pl.multiple_of((a * inner + b) * LANES, LANES), LANES)
            weights = taps[:, cols]
            pair = []
            for q in range(2):
                base = (a * 2 + q) * 2 * GROUP
                xs[base : base + GROUP, :] = lo[q, :, cols]
                xs[base + GROUP : base + 2 * GROUP, :] = hi[q, :, cols]
                total = weights[0:1] * lo[q, :, cols]
                for t in range(1, tap_count):
                    total = total + weights[t : t + 1] * xs[base + t : base + t + GROUP, :]
                pair.append(total)
            tiles_out.append(tuple(pair))
        for c, z in enumerate(transform(tiles_out)):
            at = pl.ds(pl.multiple_of((c * inner + b) * GROUP, GROUP), GROUP)
            mid[0, at, :] = z[0]
            mid[1, at, :] = z[1]
        return carry

    lax.fori_loop(0, inner, first, 0)

    for c0 in range(0, outer, 2):
        both = []
        for c in (c0, c0 + 1):
            zs = []
            for b in range(inner):
                at = slice((c * inner + b) * GROUP, (c * inner + b + 1) * GROUP)
                zs.append(times((mid[0, at, :], mid[1, at, :]), b * c, tiles))
            turned_out = []
            for d, (re, im) in enumerate(transform(zs)):
                k1 = c + outer * d
                wr, wi = tw_re[k1 : k1 + 1, :], tw_im[k1 : k1 + 1, :]
                turned_out.append((re * wr - im * wi, re * wi + im * wr))
            both.append(turned_out)
        for d in range(inner):
            at = slice((c0 + outer * d) * GROUP, (c0 + outer * d + 2) * GROUP)
            for q in range(2):
                x = jnp.concatenate([both[0][d][q], both[1][d][q]], axis=0)
                h = x.astype(jnp.bfloat16)
                rows_h[at, q * LANES : (q + 1) * LANES] = h
                rows_l[at, q * LANES : (q + 1) * LANES] = (x - h.astype(jnp.float32)).astype(jnp.bfloat16)

    def dot(x, y):
        return jnp.dot(x, y, preferred_element_type=jnp.float32)

    spec = dot(rows_h[...], high[...]) + dot(rows_l[...], high[...]) + dot(rows_h[...], low[...])
    spec_re, spec_im = spec[:, :LANES], spec[:, LANES:]
    pw[...] = spec_re * spec_re + spec_im * spec_im

    left = lax.broadcasted_iota(jnp.int32, (tiles, LANES), 1) < tiles
    total = jnp.zeros((tiles, LANES), jnp.float32)
    for f in range(0, GROUP, 2):
        pair = jnp.concatenate(
            [pw[pl.ds(f, tiles, stride=GROUP), :], pw[pl.ds(f + 1, tiles, stride=GROUP), :]], axis=0
        ).T
        upper, lower = pair[:tiles], pair[tiles:]
        one = jnp.where(left, upper, pltpu.roll(lower, tiles, 1))
        two = jnp.where(left, pltpu.roll(upper, tiles, 1), lower)
        total = total + one + two
        turned[pl.ds(f, tiles, stride=GROUP), :] = one
        turned[pl.ds(f + 1, tiles, stride=GROUP), :] = two
    return total


def kernel(beams, tms, scale, x, *refs):
    from_consts, (powers, base) = refs[:5], refs[5:7]
    refs = refs[7:]
    consts, refs = refs[:5], refs[5:]
    xv, rim, pv, tot, res, load_sem, const_sem, rim_send, rim_recv, out_sem = refs[:10]
    work, refs = refs[10:16], refs[16:]
    pols, _, frames, channels = xv.shape
    groups = frames // GROUP
    tiles = channels // LANES
    turned = work[-1]
    b, t = lax.axis_index("beam"), lax.axis_index("tm")

    loads = [pltpu.make_async_copy(x.at[p], xv.at[p], load_sem.at[p]) for p in range(pols)]
    fetches = [pltpu.make_async_copy(f, c, const_sem.at[i]) for i, (f, c) in enumerate(zip(from_consts, consts))]
    fetches[0].start()
    for copy in loads + fetches[1:]:
        copy.start()
    greet(beams, tms)
    rims = [
        remote(x.at[p, :, 0:GROUP, :], rim.at[p], rim_send.at[p], rim_recv.at[p], b, lax.rem(t + tms - 1, tms))
        for p in range(pols)
    ]

    @pl.when(t > 0)
    def _():
        for copy in rims:
            copy.start()

    @pl.when(t == tms - 1)
    def _():
        rim[...] = jnp.zeros_like(rim)

    for copy in fetches + loads:
        copy.wait()

    def one(p, g, lo, hi):
        part = channelize(lo, hi, *consts, *work)
        at = pl.ds(pl.multiple_of(p * tiles, tiles), tiles)
        if isinstance(p, int):
            tot[at, :] = tot[at, :] + part
        else:
            tot[at, :] = jnp.where(g == 0, part, tot[at, :] + part) if groups > 2 else part
        frames_at = pl.ds(pl.multiple_of(g * GROUP, GROUP), GROUP)
        for j in range(tiles):
            pv[p, frames_at, j * LANES : (j + 1) * LANES] = turned[j * GROUP : (j + 1) * GROUP, :]

    def early(i, carry):
        p, g = i // (groups - 1), lax.rem(i, groups - 1)
        after = pl.multiple_of((g + 1) * GROUP, GROUP)
        one(
            p, g,
            xv.at[p, :, pl.ds(pl.multiple_of(g * GROUP, GROUP), GROUP), :],
            xv.at[p, :, pl.ds(after, GROUP), :],
        )
        return carry

    lax.fori_loop(0, pols * (groups - 1), early, 0)

    outs = []
    totals = []
    for p in range(pols):

        @pl.when(t < tms - 1)
        def _():
            rims[p].wait_recv()

        one(p, groups - 1, xv.at[p, :, frames - GROUP : frames, :], rim.at[p])
        now = refs[p * TOTAL_SCRATCH : (p + 1) * TOTAL_SCRATCH]
        totals.append(Total(beams, tms, tot, res, p * tiles, tiles, *now[:4], now[4:]))
        totals[p].to_tm()
        outs.append(pltpu.make_async_copy(pv.at[p], powers.at[p], out_sem.at[p]))
        outs[p].start()
        if p > 0:
            totals[p - 1].back()
        totals[p].to_beams()
    for p in range(pols):
        if p == pols - 1:
            totals[p].back()
        totals[p].arrive()
        for j in range(tiles):
            row = p * tiles + j
            base[p : p + 1, j * LANES : (j + 1) * LANES] = res[row : row + 1, :] * scale
    for total in totals:
        total.leave()

    @pl.when(t > 0)
    def _():
        for copy in rims:
            copy.wait_send()

    for copy in outs:
        copy.wait()


def powers_and_base(x, taps, scale):
    beams, tms = lax.axis_size("beam"), lax.axis_size("tm")
    pols, _, frames, channels = x.shape
    tiles = channels // LANES
    rows = tiles * GROUP
    consts = (taps, *tables(channels))
    sem = pltpu.SemaphoreType.DMA
    f32 = jnp.float32
    anywhere = pl.BlockSpec(memory_space=pl.ANY)
    return pl.pallas_call(
        functools.partial(kernel, beams, tms, scale),
        out_shape=(
            jax.ShapeDtypeStruct((pols, frames, channels), f32),
            jax.ShapeDtypeStruct((pols, channels), f32),
        ),
        in_specs=[anywhere] * (1 + len(consts)),
        out_specs=(anywhere, pl.BlockSpec(memory_space=pltpu.VMEM)),
        scratch_shapes=[pltpu.VMEM(c.shape, c.dtype) for c in consts]
        + [
            pltpu.VMEM(x.shape, f32),
            pltpu.VMEM((pols, 2, GROUP, channels), f32),
            pltpu.VMEM((pols, frames, channels), f32),
            pltpu.VMEM((pols * tiles, LANES), f32),
            pltpu.VMEM((pols * tiles, LANES), f32),
            sem((pols,)), sem((len(consts),)), sem((pols,)), sem((pols,)), sem((pols,)),
            pltpu.VMEM((8 * 2 * 2 * GROUP, LANES), f32),
            pltpu.VMEM((2, rows, LANES), f32),
            pltpu.VMEM((rows, 2 * LANES), jnp.bfloat16),
            pltpu.VMEM((rows, 2 * LANES), jnp.bfloat16),
            pltpu.VMEM((rows, LANES), f32),
            pltpu.VMEM((rows, LANES), f32),
        ]
        + total_scratch(beams, tms, tiles) * pols,
        compiler_params=pltpu.CompilerParams(collective_id=0, has_side_effects=True),
        name="powers_and_base",
    )(x, *consts)


def body(voltages, filter_taps):
    frames = voltages.shape[3] * lax.axis_size("tm")
    beams = voltages.shape[0] * lax.axis_size("beam")
    powers, base = powers_and_base(voltages[0], filter_taps, 1.0 / (frames * beams))
    return (powers - base[:, None, :])[None]


def solution(mesh):
    placed = (P("beam", None, None, "tm", None), P())
    return jax.shard_map(
        body, mesh=mesh, in_specs=placed, out_specs=P("beam", None, "tm", None), check_vma=False
    )
```

time: 41.2 us -> 34.3 us (0.83)
  local copies, waits for them, and re-layouts: 3.47 us -> 0 us
  Pallas kernels: 34.8 us -> 31.9 us
  starting transfers between devices: 2.58 us -> 0 us
  other arithmetic: 0 us -> 2.28 us
    pallas_call x5 -> x1, Pallas kernels: 34.8 us -> 31.9 us  [powers_and_base(): pl.pallas_call(functools.partial(kernel, beams, tms, scale), out_shape=(j...]
    ppermute x2 -> x0, starting transfers between devices: 2.58 us -> none  [passed_along(): return lax.ppermute(x, axis, pairs)]
    broadcast_in_dim x0 -> x1, other arithmetic: none -> 2.28 us  [body(): return (powers - base[:, None, :])[None]]
    unnamed x4 -> x0, local copies, waits for them, and re-layouts: 1.58 us -> none
    slice x1 -> x0, local copies, waits for them, and re-layouts: 1.27 us -> none  [body(): segment[p:p + 1, :, :GROUP]]
    broadcast_in_dim x1 -> x0, local copies, waits for them, and re-layouts: 0.62 us -> none  [body(): total = jnp.zeros((pols, tiles, LANES), jnp.float32)]
  transfers between devices with their start and end apart: 2 -> 0, of which waited for: 0 -> 0; matrix products, arithmetic and copies ran while one was open for 2% -> 0% of each run, Pallas kernels for 22% -> 0%
where the time goes in v3:
time: 34.3 us; the launch traced here: 34.2 us
  Pallas kernels  31.9 us (93%)
  other arithmetic  2.28 us (7%)
    pallas_call x1, Pallas kernels, powers_and_base(): pl.pallas_call(functools.partial(kernel, beams, tms, scale), out_shape=(j...  31.9 us
    broadcast_in_dim x1, other arithmetic, body(): return (powers - base[:, None, :])[None]  2.28 us

profile of v3, /device:TPU:0, one launch (start us, length us, event | category | flops | bytes accessed | tf_op | source)
XLA Modules:
  0.0 34.2 jit_solution(14325613365774449934)
XLA Ops:
  0.0 31.9 %powers_and_base.1 = (f32[2,16,8192]{2,1,0:T(8,128)}, f32[2,8192]{1,0:T(2,128)}) custom-call(f32[2,2,16,8192]{3,2,1,0:T(8,128)} %bitcast.3, f32[8,8192]{1,0:T(8,128)} %refs_0_.1, f32[64,128]{1,0:T(8,128)} %constant.7.clone.refs_1_, f32[64,128]{1,0:T(8,128)} %constant.8.clone.refs_2_, bf16[256,256]{1,0:T(8,128)(2,1)} %constant.10.refs_3_, ...), custom_call_target="tpu_custom_call" | custom-call | tf_op jit(solution)/shard_map/powers_and_base/pallas_call | solution.py:337
  31.9 2.3 %subtract_bitcast_fusion = f32[1,2,16,8192]{3,2,1,0:T(8,128)} fusion(f32[2,16,8192]{2,1,0:T(8,128)} %get-tuple-element.7, f32[2,8192]{1,0:T(2,128)} %get-tuple-element.8), kind=kLoop, calls=%fused_computation | loop fusion | flops 262144 | bytes 2162688 | tf_op jit(solution)/shard_map/broadcast_in_dim | solution.py:370

commit v4 on v3

--- a/solution.py
+++ b/solution.py
@@ -241,6 +241,7 @@
     groups = frames // GROUP
     tiles = channels // LANES
     turned = work[-1]
+    reach = consts[0].shape[0] - 1
     b, t = lax.axis_index("beam"), lax.axis_index("tm")
 
     loads = [pltpu.make_async_copy(x.at[p], xv.at[p], load_sem.at[p]) for p in range(pols)]
@@ -250,7 +251,7 @@
         copy.start()
     greet(beams, tms)
     rims = [
-        remote(x.at[p, :, 0:GROUP, :], rim.at[p], rim_send.at[p], rim_recv.at[p], b, lax.rem(t + tms - 1, tms))
+        remote(x.at[p, :, 0:reach, :], rim.at[p, :, 0:reach, :], rim_send.at[p], rim_recv.at[p], b, lax.rem(t + tms - 1, tms))
         for p in range(pols)
     ]
 
@@ -340,7 +341,7 @@
             jax.ShapeDtypeStruct((pols, frames, channels), f32),
             jax.ShapeDtypeStruct((pols, channels), f32),
         ),
-        in_specs=[anywhere] * (1 + len(consts)),
+        in_specs=[pl.BlockSpec(memory_space=pltpu.HBM)] * (1 + len(consts)),
         out_specs=(anywhere, pl.BlockSpec(memory_space=pltpu.VMEM)),
         scratch_shapes=[pltpu.VMEM(c.shape, c.dtype) for c in consts]
         + [
@@ -358,7 +359,9 @@
             pltpu.VMEM((rows, LANES), f32),
         ]
         + total_scratch(beams, tms, tiles) * pols,
-        compiler_params=pltpu.CompilerParams(collective_id=0, has_side_effects=True),
+        compiler_params=pltpu.CompilerParams(
+            collective_id=0, has_side_effects=True
+        ),
         name="powers_and_base",
     )(x, *consts)
 

time: 34.3 us -> 32.9 us (0.959)
  Pallas kernels: 31.9 us -> 30.5 us
    pallas_call x1, Pallas kernels: 31.9 us -> 30.5 us  [powers_and_base(): pl.pallas_call(functools.partial(kernel, beams, tms, scale), out_shape=(j...]
where the time goes in v4:
time: 32.9 us; the launch traced here: 32.8 us
  Pallas kernels  30.5 us (93%)
  other arithmetic  2.28 us (7%)
    pallas_call x1, Pallas kernels, powers_and_base(): pl.pallas_call(functools.partial(kernel, beams, tms, scale), out_shape=(j...  30.5 us
    broadcast_in_dim x1, other arithmetic, body(): return (powers - base[:, None, :])[None]  2.28 us

profile of v4, /device:TPU:0, one launch (start us, length us, event | category | flops | bytes accessed | tf_op | source)
XLA Modules:
  0.0 32.8 jit_solution(6253838763723713221)
XLA Ops:
  0.0 30.5 %powers_and_base.1 = (f32[2,16,8192]{2,1,0:T(8,128)}, f32[2,8192]{1,0:T(2,128)}) custom-call(f32[2,2,16,8192]{3,2,1,0:T(8,128)} %bitcast.3, f32[8,8192]{1,0:T(8,128)} %refs_0_.1, f32[64,128]{1,0:T(8,128)} %constant.7.clone.refs_1_, f32[64,128]{1,0:T(8,128)} %constant.8.clone.refs_2_, bf16[256,256]{1,0:T(8,128)(2,1)} %constant.10.refs_3_, ...), custom_call_target="tpu_custom_call" | custom-call | tf_op jit(solution)/shard_map/powers_and_base/pallas_call | solution.py:338
  30.5 2.3 %subtract_bitcast_fusion = f32[1,2,16,8192]{3,2,1,0:T(8,128)} fusion(f32[2,16,8192]{2,1,0:T(8,128)} %get-tuple-element.7, f32[2,8192]{1,0:T(2,128)} %get-tuple-element.8), kind=kLoop, calls=%fused_computation | loop fusion | flops 262144 | bytes 2162688 | tf_op jit(solution)/shard_map/broadcast_in_dim | solution.py:373

commit v5 on v4

--- a/solution.py
+++ b/solution.py
@@ -246,25 +246,23 @@
 
     loads = [pltpu.make_async_copy(x.at[p], xv.at[p], load_sem.at[p]) for p in range(pols)]
     fetches = [pltpu.make_async_copy(f, c, const_sem.at[i]) for i, (f, c) in enumerate(zip(from_consts, consts))]
-    fetches[0].start()
-    for copy in loads + fetches[1:]:
+    for copy in loads + fetches:
         copy.start()
     greet(beams, tms)
     rims = [
-        remote(x.at[p, :, 0:reach, :], rim.at[p, :, 0:reach, :], rim_send.at[p], rim_recv.at[p], b, lax.rem(t + tms - 1, tms))
+        remote(xv.at[p, :, 0:reach, :], rim.at[p, :, 0:reach, :], rim_send.at[p], rim_recv.at[p], b, lax.rem(t + tms - 1, tms))
         for p in range(pols)
     ]
 
-    @pl.when(t > 0)
-    def _():
-        for copy in rims:
-            copy.start()
+    for load, copy in zip(loads, rims):
+        load.wait()
+        pl.when(t > 0)(copy.start)
 
     @pl.when(t == tms - 1)
     def _():
         rim[...] = jnp.zeros_like(rim)
 
-    for copy in fetches + loads:
+    for copy in fetches:
         copy.wait()
 
     def one(p, g, lo, hi):

time: 32.9 us -> 32.9 us (level)
  no operation moved by 1% of the time
where the time goes in v5:
time: 32.9 us; the launch traced here: 32.7 us
  Pallas kernels  30.4 us (92%)
  other arithmetic  2.28 us (7%)
    pallas_call x1, Pallas kernels, powers_and_base(): pl.pallas_call(functools.partial(kernel, beams, tms, scale), out_shape=(j...  30.4 us
    broadcast_in_dim x1, other arithmetic, body(): return (powers - base[:, None, :])[None]  2.28 us

profile of v5, /device:TPU:0, one launch (start us, length us, event | category | flops | bytes accessed | tf_op | source)
XLA Modules:
  0.0 32.7 jit_solution(16952605269758369747)
XLA Ops:
  0.0 30.4 %powers_and_base.1 = (f32[2,16,8192]{2,1,0:T(8,128)}, f32[2,8192]{1,0:T(2,128)}) custom-call(f32[2,2,16,8192]{3,2,1,0:T(8,128)} %bitcast.3, f32[8,8192]{1,0:T(8,128)} %refs_0_.1, f32[64,128]{1,0:T(8,128)} %constant.7.clone.refs_1_, f32[64,128]{1,0:T(8,128)} %constant.8.clone.refs_2_, bf16[256,256]{1,0:T(8,128)(2,1)} %constant.10.refs_3_, ...), custom_call_target="tpu_custom_call" | custom-call | tf_op jit(solution)/shard_map/powers_and_base/pallas_call | solution.py:336
  30.4 2.3 %subtract_bitcast_fusion = f32[1,2,16,8192]{3,2,1,0:T(8,128)} fusion(f32[2,16,8192]{2,1,0:T(8,128)} %get-tuple-element.7, f32[2,8192]{1,0:T(2,128)} %get-tuple-element.8), kind=kLoop, calls=%fused_computation | loop fusion | flops 262144 | bytes 2162688 | tf_op jit(solution)/shard_map/broadcast_in_dim | solution.py:371
